TPU v7x, 32 devices: a whole 2x2x4 slice. The times are simulated.
32 devices in a mesh: seq: 16 (over z, y, x), tp: 2 (over core).
Axes of the slice: x: 2, y: 2, z: 4, core: 2. Of those that a mesh axis runs over, the one named last changes fastest.
Arguments:
- inner_input: bfloat16 [4096, 2560], P('seq', 'tp'), may hold values from -6 to 6
- gate_input: bfloat16 [4096, 2560], P('seq', 'tp'), may hold values from -170 to 170
- state_input: bfloat16 [4096, 256], P('seq'), may hold values from -6 to 6
- step_raw: float32 [40, 4096], P('tp', 'seq'), may hold values from -14 to 0
- conv_inner: float32 [4, 2560], P(None, 'tp'), may hold values from -3 to 3
- conv_state: float32 [4, 256], replicated, may hold values from -3 to 3
- bias_inner: float32 [2560], P('tp'), may hold values from -3 to 3
- bias_state: float32 [256], replicated, may hold values from -3 to 3
- step_bias: float32 [40], P('tp'), may hold values from -0.3 to 0.3
- decay_log: float32 [40], P('tp'), may hold values from -1.4 to 0
- skip_gain: float32 [40], P('tp'), may hold values from 0.5 to 1.5
- norm_gain: float32 [2560], P('tp'), may hold values from 0.1 to 1.9
- out_weight: bfloat16 [2560, 2560], P('tp'), may hold values from -0.15625 to 0.15625
Outputs:
- block_out: bfloat16 [4096, 2560], P('seq', 'tp')
All inputs are finite; a program needn't handle non-finite values.
Results may differ from a plain program's by a relative error of at most 0.008.
Values may be sent and summed in bfloat16 or wider, within the bound.
A program may use at most 64 MiB of HBM per device.

v0:
```python
import functools

import jax
import jax.numpy as jnp
from jax import lax
from jax.experimental import pallas as pl
from jax.experimental.pallas import tpu as pltpu
from jax.sharding import PartitionSpec as P

HEAD_DIM = 64
NSTATE = 128
LANES = 128
GROUP = 32
RIM = 8
MESH = pl.DeviceIdType.MESH
f32 = jnp.float32
bf16 = jnp.bfloat16


def silu(v):
    return v / (1.0 + jnp.exp(-v))


def log1p_exp(v):
    u = jnp.exp(-jnp.abs(v))
    z = u / (2.0 + u)
    q = z * z
    series = jnp.full_like(q, 1.0 / 19.0)
    for odd in range(17, 0, -2):
        series = series * q + 1.0 / odd
    return jnp.maximum(v, 0.0) + 2.0 * z * series


def spread_heads(table, ones):
    high = table.astype(bf16)
    low = (table - high.astype(f32)).astype(bf16)
    out = jnp.dot(high, ones, preferred_element_type=f32)
    return out + jnp.dot(low, ones, preferred_element_type=f32)


def conv_rows(src, taps, bias, start, rows, columns):
    count = taps.shape[0]
    total = bias[...]
    for k in range(count):
        first = start + RIM - count + 1 + k
        total = total + taps[k : k + 1] * src[pl.ds(first, rows), columns]
    return silu(total)


def kernel(
    n,
    x_hbm, gate_hbm, state_in, step_raw, taps_x, taps_s, bias_x, bias_s,
    step_bias, decay_log, skip_gain, norm_gain, w_hbm,
    out_ref,
    x_in, gate_in, w_all, x_pad, s_pad, x_conv, s_conv, table, spread, cols,
    scores, mixed, gate_act, decayed, gated,
    rim_x, rim_s, decay_out, decay_all, decay_cols,
    full, slices, got1, back, got2, entering,
    part, part_got, own, squares, squares_got,
    load_sem, rim_send, rim_recv, d_send, d_recv, s1_send, s1_recv,
    s2_send, s2_recv, o_send, o_recv, q_sem,
):
    me = lax.axis_index("seq")
    core = lax.axis_index("tp")
    other = 1 - core
    rows, inner = x_in.shape
    heads = step_raw.shape[0]
    tiles = inner // LANES
    per = NSTATE // n
    slot = slices.shape[2]
    wide = inner // 2
    half = rows // 2

    barrier = pltpu.get_barrier_semaphore()

    def greet(k, _):
        pl.semaphore_signal(
            barrier, inc=1, device_id={"seq": lax.rem(me + k, n)}, device_id_type=MESH
        )
        return 0

    lax.fori_loop(1, n, greet, 0)
    pl.semaphore_signal(barrier, inc=1, device_id={"tp": other}, device_id_type=MESH)

    load_x = pltpu.make_async_copy(x_hbm, x_in, load_sem.at[0])
    load_g = pltpu.make_async_copy(gate_hbm, gate_in, load_sem.at[1])
    load_w = pltpu.make_async_copy(w_hbm, w_all, load_sem.at[2])
    load_x.start()
    load_g.start()
    load_w.start()

    eye = (
        lax.broadcasted_iota(jnp.int32, (heads, heads), 0)
        == lax.broadcasted_iota(jnp.int32, (heads, heads), 1)
    )

    def as_column(row):
        return jnp.sum(jnp.where(eye, row[...], 0.0), axis=1, keepdims=True)

    step = log1p_exp(step_raw[...] + as_column(step_bias))
    log_decay = -jnp.exp(as_column(decay_log)) * step
    upper = (
        lax.broadcasted_iota(jnp.int32, (rows, rows), 0)
        <= lax.broadcasted_iota(jnp.int32, (rows, rows), 1)
    ).astype(f32)
    cum = jnp.dot(
        log_decay, upper, precision=lax.Precision.HIGHEST, preferred_element_type=f32
    )
    shifted = cum - jnp.log(step)
    table[...] = jnp.zeros_like(table)
    table[0:heads] = cum
    table[GROUP : GROUP + heads] = jnp.exp(cum[:, rows - 1 : rows] - shifted)
    table[2 * GROUP : 2 * GROUP + heads] = jnp.exp(cum)
    flipped = table[...].T
    cols[...] = flipped
    lane = lax.broadcasted_iota(jnp.int32, (1, LANES), 1) // GROUP
    decay_out[...] = jnp.where(
        lane == 2, jnp.broadcast_to(flipped[rows - 1 : rows], (8, LANES)), 0.0
    )
    decay_all[me] = decay_out[...]

    def rim_copies():
        target = {"seq": lax.rem(me + 1, n)}
        return [
            pltpu.make_async_remote_copy(
                src_ref=src.at[pl.ds(rows - RIM, RIM)],
                dst_ref=dst,
                send_sem=rim_send.at[i],
                recv_sem=rim_recv.at[i],
                device_id=target,
                device_id_type=MESH,
            )
            for i, (src, dst) in enumerate(((x_hbm, rim_x), (state_in, rim_s)))
        ]

    spread[...] = jnp.where(
        lax.broadcasted_iota(jnp.int32, (LANES, inner), 0) % GROUP
        == lax.broadcasted_iota(jnp.int32, (LANES, inner), 1) // HEAD_DIM,
        1.0,
        0.0,
    ).astype(bf16)

    s_pad[0:RIM] = jnp.zeros((RIM, s_pad.shape[1]), f32)
    s_pad[RIM:] = state_in[...].astype(f32)
    s_conv[...] = conv_rows(s_pad, taps_s, bias_s, 0, rows, slice(None)).astype(bf16)
    x_pad[0:RIM] = jnp.zeros((RIM, inner), f32)
    load_x.wait()
    for i in range(tiles):
        c = slice(i * LANES, (i + 1) * LANES)
        x_pad[RIM:, c] = x_in[:, c].astype(f32)
        x_conv[:, c] = conv_rows(
            x_pad, taps_x[:, c], bias_x[i : i + 1], 0, rows, c
        ).astype(bf16)

    pl.semaphore_wait(barrier, n)

    @pl.when(me < n - 1)
    def _():
        for copy in rim_copies():
            copy.start()

    def decay_copy(k):
        to = lax.rem(me + k, n)
        return pltpu.make_async_remote_copy(
            src_ref=decay_out,
            dst_ref=decay_all.at[me],
            send_sem=d_send.at[k],
            recv_sem=d_recv.at[me],
            device_id={"seq": to},
            device_id_type=MESH,
        )

    def decay_start(k, _):
        decay_copy(k).start()
        return 0

    lax.fori_loop(1, n, decay_start, 0)

    load_g.wait()
    carry_decay = jnp.where(lane == 2, cols[...], 0.0)
    for i in range(tiles):
        c = slice(i * LANES, (i + 1) * LANES)
        gate_act[:, c] = silu(gate_in[:, c].astype(f32))
        decayed[:, c] = spread_heads(carry_decay, spread[:, c])

    @pl.when(me > 0)
    def _():
        for copy in rim_copies():
            copy.wait_recv()
        s_pad[0:RIM] = rim_s[...].astype(f32)
        x_pad[0:RIM] = rim_x[...].astype(f32)

    s_conv[0:16] = conv_rows(s_pad, taps_s, bias_s, 0, 16, slice(None)).astype(bf16)
    for i in range(tiles):
        c = slice(i * LANES, (i + 1) * LANES)
        x_conv[0:16, c] = conv_rows(
            x_pad, taps_x[:, c], bias_x[i : i + 1], 0, 16, c
        ).astype(bf16)

    def state_copy(part_no, k):
        to = lax.rem(me + k, n)
        return pltpu.make_async_remote_copy(
            src_ref=slices.at[part_no, to],
            dst_ref=got1.at[part_no, me],
            send_sem=s1_send.at[part_no, k],
            recv_sem=s1_recv.at[part_no, me],
            device_id={"seq": to},
            device_id_type=MESH,
        )

    towards = jnp.where(lane == 1, cols[...], 0.0)
    for b in range(2):
        for i in range(b * tiles // 2, (b + 1) * tiles // 2):
            c = slice(i * LANES, (i + 1) * LANES)
            scaled = (
                x_conv[:, c].astype(f32) * spread_heads(towards, spread[:, c])
            ).astype(bf16)
            full[:, c] = lax.dot_general(
                s_conv[:, :NSTATE], scaled, (((0,), (0,)), ((), ())),
                preferred_element_type=f32,
            )

        def cut(j, _, b=b):
            piece = full[
                pl.ds(pl.multiple_of(j * per, per), per), b * wide : (b + 1) * wide
            ]
            slices[b, j] = jnp.broadcast_to(piece, (slot, wide)).astype(bf16)
            return 0

        lax.fori_loop(0, n, cut, 0)

        @pl.when(me < n - 1)
        def _(b=b):
            def start(k, _):
                state_copy(b, k).start()
                return 0

            lax.fori_loop(1, n, start, 0)

        got1[b, me] = slices[b, me]

    def decay_wait(k, _):
        source = lax.rem(me + k, n)
        pltpu.make_async_remote_copy(
            src_ref=decay_out,
            dst_ref=decay_all.at[source],
            send_sem=d_send.at[k],
            recv_sem=d_recv.at[source],
            device_id={"seq": source},
            device_id_type=MESH,
        ).wait_recv()
        return 0

    lax.fori_loop(1, n, decay_wait, 0)
    decay_cols[...] = spread_heads(
        decay_all[...].reshape(n * 8, LANES), spread[...]
    ).reshape(n, 8, inner)

    keys = s_conv[:, :NSTATE]
    query = s_conv[:, NSTATE:]
    causal = (
        lax.broadcasted_iota(jnp.int32, (rows, rows), 0)
        >= lax.broadcasted_iota(jnp.int32, (rows, rows), 1)
    )
    scores[...] = jnp.where(
        causal,
        lax.dot_general(
            query, keys, (((1,), (1,)), ((), ())), preferred_element_type=f32
        ),
        0.0,
    )
    first_half = lax.broadcasted_iota(jnp.int32, (1, LANES), 1) < HEAD_DIM

    def inside(i):
        c = slice(i * LANES, (i + 1) * LANES)
        x_c = x_conv[:, c]
        tops, bottoms = [], []
        for h in (2 * i, 2 * i + 1):
            a_row = shifted[h : h + 1, :]
            top = cols[0:half, h : h + 1] - a_row[:, :half]
            top = scores[0:half, 0:half] * jnp.exp(jnp.minimum(top, 80.0))
            tops.append(
                jnp.dot(top.astype(bf16), x_c[:half], preferred_element_type=f32)
            )
            low = cols[half:, h : h + 1] - a_row
            low = scores[half:, :] * jnp.exp(jnp.minimum(low, 80.0))
            bottoms.append(jnp.dot(low.astype(bf16), x_c, preferred_element_type=f32))
        gain = jnp.where(
            first_half,
            skip_gain[:, 2 * i : 2 * i + 1],
            skip_gain[:, 2 * i + 1 : 2 * i + 2],
        )
        x_f = x_c.astype(f32)
        mixed[0:half, c] = jnp.where(first_half, *tops) + gain * x_f[:half]
        mixed[half:, c] = jnp.where(first_half, *bottoms) + gain * x_f[half:]

    for i in range(tiles):
        inside(i)

    def back_copy(b, k):
        to = lax.rem(me + k, n)
        return to, pltpu.make_async_remote_copy(
            src_ref=back.at[b, to],
            dst_ref=got2.at[b, me],
            send_sem=s2_send.at[b, k],
            recv_sem=s2_recv.at[b, me],
            device_id={"seq": to},
            device_id_type=MESH,
        )

    for b in range(2):
        c = slice(b * wide, (b + 1) * wide)

        def prefix(j, state, b=b, c=c):
            back[b, j] = state.astype(bf16)

            @pl.when(j != me)
            def _():
                pltpu.make_async_remote_copy(
                    src_ref=slices.at[b, j],
                    dst_ref=got1.at[b, j],
                    send_sem=s1_send.at[b, 0],
                    recv_sem=s1_recv.at[b, j],
                    device_id={"seq": lax.rem(me + 1, n)},
                    device_id_type=MESH,
                ).wait_recv()

            return decay_cols[j][0:1, c] * state + got1[b, j].astype(f32)

        state = lax.fori_loop(0, n - 1, prefix, jnp.zeros((slot, wide), f32))
        back[b, n - 1] = state.astype(bf16)

        def back_start(k, _, b=b):
            to, copy = back_copy(b, k)

            @pl.when(to > 0)
            def _():
                copy.start()

            return 0

        lax.fori_loop(1, n, back_start, 0)
        got2[b, me] = back[b, me]

    @pl.when(me > 0)
    def _():
        for b in range(2):

            def back_wait(k, _, b=b):
                source = lax.rem(me + k, n)
                pltpu.make_async_remote_copy(
                    src_ref=back.at[b, source],
                    dst_ref=got2.at[b, source],
                    send_sem=s2_send.at[b, k],
                    recv_sem=s2_recv.at[b, source],
                    device_id={"seq": source},
                    device_id_type=MESH,
                ).wait_recv()
                return 0

            lax.fori_loop(1, n, back_wait, 0)

            def place(j, _, b=b):
                entering[
                    pl.ds(pl.multiple_of(j * per, per), per), b * wide : (b + 1) * wide
                ] = got2[b, j].astype(f32)[0:per]
                return 0

            lax.fori_loop(0, n, place, 0)

    @pl.when(me == 0)
    def _():
        entering[...] = jnp.zeros_like(entering)

    total = jnp.zeros((rows, LANES), f32)
    for i in range(tiles):
        c = slice(i * LANES, (i + 1) * LANES)
        carried = jnp.dot(
            query, entering[:, c].astype(bf16), preferred_element_type=f32
        )
        raw = (mixed[:, c] + carried * decayed[:, c]) * gate_act[:, c]
        total = total + raw * raw
        gated[:, c] = (raw * norm_gain[i : i + 1]).astype(bf16)
    squares[...] = total

    def across(src, dst, send, recv):
        return pltpu.make_async_remote_copy(
            src_ref=src,
            dst_ref=dst,
            send_sem=send,
            recv_sem=recv,
            device_id={"tp": other},
            device_id_type=MESH,
        )

    copy_q = across(squares, squares_got, q_sem.at[0], q_sem.at[1])
    copy_q.start()
    load_w.wait()
    pieces, _, width = part.shape

    def part_copy(p):
        return across(part.at[p], part_got.at[p], o_send.at[p], o_recv.at[p])

    for p in range(pieces):
        at = pl.ds(pl.multiple_of(other * inner + p * width, LANES), width)
        part[p] = jnp.dot(
            gated[...], w_all[:, at], preferred_element_type=f32
        ).astype(bf16)
        part_copy(p).start()
    for p in range(pieces):
        at = pl.ds(pl.multiple_of(core * inner + p * width, LANES), width)
        own[p] = jnp.dot(gated[...], w_all[:, at], preferred_element_type=f32)
    copy_q.wait_recv()
    both = jnp.sum(squares[...] + squares_got[...], axis=1, keepdims=True)
    scale = lax.rsqrt(both / (2 * inner) + 1e-05)
    for p in range(pieces):
        part_copy(p).wait_recv()
        out_ref[:, p * width : (p + 1) * width] = (
            (own[p] + part_got[p].astype(f32)) * scale
        ).astype(bf16)

    copy_q.wait_send()
    for p in range(pieces):
        part_copy(p).wait_send()

    def drain(k, _):
        decay_copy(k).wait_send()
        for b in range(2):
            to, copy = back_copy(b, k)

            @pl.when(to > 0)
            def _(copy=copy):
                copy.wait_send()

        return 0

    lax.fori_loop(1, n, drain, 0)

    @pl.when(me < n - 1)
    def _():
        for copy in rim_copies():
            copy.wait_send()

        def drain1(k, _):
            state_copy(0, k).wait_send()
            state_copy(1, k).wait_send()
            return 0

        lax.fori_loop(1, n, drain1, 0)


def local(
    inner_input, gate_input, state_input, step_raw, conv_inner, conv_state,
    bias_inner, bias_state, step_bias, decay_log, skip_gain, norm_gain, out_weight,
):
    n = lax.axis_size("seq")
    rows, inner = inner_input.shape
    maps = state_input.shape[1]
    slot = max(8, NSTATE // n)
    width = 256
    pieces = inner // width
    vm = pltpu.VMEM
    dma = pltpu.SemaphoreType.DMA
    any_spec = pl.BlockSpec(memory_space=pltpu.HBM)
    vmem_spec = pl.BlockSpec(memory_space=pltpu.VMEM)
    scratch = [
        vm((rows, inner), bf16),
        vm((rows, inner), bf16),
        vm(out_weight.shape, bf16),
        vm((rows + RIM, inner), f32),
        vm((rows + RIM, maps), f32),
        vm((rows, inner), bf16),
        vm((rows, maps), bf16),
        vm((LANES, rows), f32),
        vm((LANES, inner), bf16),
        vm((rows, LANES), f32),
        vm((rows, rows), f32),
        vm((rows, inner), f32),
        vm((rows, inner), f32),
        vm((rows, inner), f32),
        vm((rows, inner), bf16),
        vm((RIM, inner), bf16),
        vm((RIM, maps), bf16),
        vm((8, LANES), f32),
        vm((n, 8, LANES), f32),
        vm((n, 8, inner), f32),
        vm((NSTATE, inner), f32),
        vm((2, n, slot, inner // 2), bf16),
        vm((2, n, slot, inner // 2), bf16),
        vm((2, n, slot, inner // 2), bf16),
        vm((2, n, slot, inner // 2), bf16),
        vm((NSTATE, inner), f32),
        vm((pieces, rows, width), bf16),
        vm((pieces, rows, width), bf16),
        vm((pieces, rows, width), f32),
        vm((rows, LANES), f32),
        vm((rows, LANES), f32),
        dma((3,)), dma((2,)), dma((2,)),
        dma((n,)), dma((n,)), dma((2, n)), dma((2, n)), dma((2, n)), dma((2, n)),
        dma((pieces,)), dma((pieces,)), dma((2,)),
    ]
    row = lambda v: v.reshape(1, -1)
    tile = lambda v: v.reshape(-1, LANES)
    return pl.pallas_call(
        functools.partial(kernel, n),
        out_shape=jax.ShapeDtypeStruct((rows, inner), bf16),
        in_specs=[any_spec, any_spec] + [vmem_spec] * 10 + [any_spec],
        out_specs=vmem_spec,
        scratch_shapes=scratch,
        compiler_params=pltpu.CompilerParams(
            collective_id=0, has_side_effects=True, vmem_limit_bytes=58 * 2**20
        ),
        name="ssd_block",
    )(
        inner_input, gate_input, state_input, step_raw, conv_inner, conv_state,
        tile(bias_inner), row(bias_state), row(step_bias), row(decay_log),
        row(skip_gain), tile(norm_gain), out_weight,
    )


def solution(mesh):
    return jax.shard_map(
        local,
        mesh=mesh,
        in_specs=(
            P("seq", "tp"),
            P("seq", "tp"),
            P("seq", None),
            P("tp", "seq"),
            P(None, "tp"),
            P(),
            P("tp"),
            P(),
            P("tp"),
            P("tp"),
            P("tp"),
            P("tp"),
            P("tp", None),
        ),
        out_specs=P("seq", "tp"),
        check_vma=False,
    )
```

profile of v0, /device:TPU:3, one launch (start us, length us, event | category | flops | bytes accessed | tf_op | source)
XLA Modules:
  0.0 36.9 jit_solution(908819315538650668)
XLA Ops:
  0.0 34.9 %ssd_block.1 = bf16[256,1280]{1,0:T(8,128)(2,1)} custom-call(bf16[256,1280]{1,0:T(8,128)(2,1)} %x_hbm.1, bf16[256,1280]{1,0:T(8,128)(2,1)} %gate_hbm.1, bf16[256,256]{1,0:T(8,128)(2,1)} %state_in.1, f32[20,256]{1,0:T(8,128)} %step_raw.1, f32[4,1280]{1,0:T(4,128)} %taps_x.1, f32[4,256]{1,0:T(4,128)} %taps_s.1, f32[10,128]{1,0:T(8,128)} %bitcast.6, ...), custom_call_target="tpu_custom_call" | custom-call | tf_op jit(solution)/shard_map/ssd_block/pallas_call | solution.py:504
  34.9 2.0 %copy.15 = bf16[256,1280]{1,0:T(8,128)(2,1)} copy(bf16[256,1280]{1,0:T(8,128)(2,1)} %ssd_block.1) | data formatting | bytes 1310720
where the time goes:
time: 37 us; the launch traced here: 36.9 us
  Pallas kernels  34.9 us (94%)
  local copies, waits for them, and re-layouts  1.97 us (5%)
    pallas_call x1, Pallas kernels, local(): pl.pallas_call(functools.partial(kernel, n), out_shape=jax.ShapeDtypeStru...  34.9 us
    unnamed x1, local copies, waits for them, and re-layouts  1.97 us

commit v1 on v0

v1 whole, which is shorter than its diff:
```python
import functools
import math

import jax
import jax.numpy as jnp
from jax import lax
from jax.experimental import pallas as pl
from jax.experimental.pallas import tpu as pltpu
from jax.sharding import PartitionSpec as P

HEAD_DIM = 64
NSTATE = 128
LANES = 128
GROUP = 32
RIM = 8
HEAD = 16
MESH = pl.DeviceIdType.MESH
f32 = jnp.float32
bf16 = jnp.bfloat16


def silu(v):
    return v / (1.0 + jnp.exp(-v))


def log1p_exp(v):
    u = jnp.exp(-jnp.abs(v))
    z = u / (2.0 + u)
    q = z * z
    series = jnp.full_like(q, 1.0 / 19.0)
    for odd in range(17, 0, -2):
        series = series * q + 1.0 / odd
    return jnp.maximum(v, 0.0) + 2.0 * z * series


def spread_heads(table, ones):
    high = table.astype(bf16)
    low = (table - high.astype(f32)).astype(bf16)
    out = jnp.dot(high, ones, preferred_element_type=f32)
    return out + jnp.dot(low, ones, preferred_element_type=f32)


def conv_rows(src, taps, bias, start, rows, columns):
    count = taps.shape[0]
    total = bias[...]
    for k in range(count):
        first = start + RIM - count + 1 + k
        total = total + taps[k : k + 1] * src[pl.ds(first, rows), columns]
    return silu(total)


def wait_for(ref, sem):
    pltpu.make_async_copy(ref, ref, sem).wait()


def remote(src, dst, send, recv, to):
    return pltpu.make_async_remote_copy(
        src_ref=src,
        dst_ref=dst,
        send_sem=send,
        recv_sem=recv,
        device_id=to,
        device_id_type=MESH,
    )


def split_columns(inner):
    first = -(-inner * 3 // 5 // 256) * 256
    return ((0, first), (first, inner - first))


def kernel(
    n, g,
    x_hbm, gate_hbm, state_hbm, step_hbm, taps_x_hbm, taps_s_hbm, bias_x_hbm,
    bias_s_hbm, step_bias_hbm, decay_log_hbm, skip_gain_hbm, norm_gain_hbm, w_hbm,
    out_ref,
    x_in, gate_in, state_in, step_raw, taps_x, taps_s, bias_x, bias_s,
    step_bias, decay_log, skip_gain, norm_gain, w_all,
    x_pad, s_pad, x_conv, s_conv, table, spread, cols,
    scores, mixed, gate_act, decayed, gated, main,
    rim_x, rim_s, decay_out, decay_all, decay_cols, reach,
    out0, out1, got0, got1, before0, before1, back0, back1, ent0, ent1,
    pass0, pass1, in0, in1,
    acc, part, part_got, squares, squares_got,
    load_sem, rim_send, rim_recv, d_send, d_recv, s1_send, s1_recv,
    s2_send, s2_recv, c_send, c_recv, o_send, o_recv, q_sem,
):
    me = lax.axis_index("seq")
    core = lax.axis_index("tp")
    other = 1 - core
    rows, inner = x_in.shape
    heads = step_raw.shape[0]
    tiles = inner // LANES
    per = NSTATE // g
    half = rows // 2
    mg = lax.rem(me, g)
    base = me - mg
    columns = split_columns(inner)
    part_refs = (
        (out0, got0, before0, back0, ent0, pass0, in0),
        (out1, got1, before1, back1, ent1, pass1, in1),
    )

    barrier = pltpu.get_barrier_semaphore()

    def greet(k, _):
        pl.semaphore_signal(
            barrier,
            inc=1,
            device_id={"seq": base + lax.rem(mg + k, g)},
            device_id_type=MESH,
        )
        return 0

    lax.fori_loop(1, g, greet, 0)
    pl.semaphore_signal(barrier, inc=1, device_id={"tp": other}, device_id_type=MESH)

    @pl.when(me >= g)
    def _():
        pl.semaphore_signal(
            barrier, inc=1, device_id={"seq": me - g}, device_id_type=MESH
        )

    @pl.when((me >= g) & (mg == 0))
    def _():
        pl.semaphore_signal(
            barrier, inc=1, device_id={"seq": me - 1}, device_id_type=MESH
        )

    pairs = (
        (x_hbm, x_in), (state_hbm, state_in), (step_hbm, step_raw),
        (step_bias_hbm, step_bias), (decay_log_hbm, decay_log),
        (taps_s_hbm, taps_s), (bias_s_hbm, bias_s), (taps_x_hbm, taps_x),
        (bias_x_hbm, bias_x), (skip_gain_hbm, skip_gain),
        (norm_gain_hbm, norm_gain), (gate_hbm, gate_in), (w_hbm, w_all),
    )
    loads = [
        pltpu.make_async_copy(src, dst, load_sem.at[i])
        for i, (src, dst) in enumerate(pairs)
    ]
    for load in loads:
        load.start()

    spread[...] = jnp.where(
        lax.broadcasted_iota(jnp.int32, (LANES, inner), 0) % GROUP
        == lax.broadcasted_iota(jnp.int32, (LANES, inner), 1) // HEAD_DIM,
        1.0,
        0.0,
    ).astype(bf16)
    eye = (
        lax.broadcasted_iota(jnp.int32, (heads, heads), 0)
        == lax.broadcasted_iota(jnp.int32, (heads, heads), 1)
    )

    def as_column(row):
        return jnp.sum(jnp.where(eye, row[...], 0.0), axis=1, keepdims=True)

    for load in loads[2:5]:
        load.wait()
    step = log1p_exp(step_raw[...] + as_column(step_bias))
    log_decay = -jnp.exp(as_column(decay_log)) * step
    upper = (
        lax.broadcasted_iota(jnp.int32, (rows, rows), 0)
        <= lax.broadcasted_iota(jnp.int32, (rows, rows), 1)
    ).astype(f32)
    cum = jnp.dot(
        log_decay, upper, precision=lax.Precision.HIGHEST, preferred_element_type=f32
    )
    shifted = cum - jnp.log(step)
    table[...] = jnp.zeros_like(table)
    table[0:heads] = cum
    table[GROUP : GROUP + heads] = jnp.exp(cum[:, rows - 1 : rows] - shifted)
    table[2 * GROUP : 2 * GROUP + heads] = jnp.exp(cum)
    flipped = table[...].T
    cols[...] = flipped
    lane = lax.broadcasted_iota(jnp.int32, (1, LANES), 1) // GROUP
    decay_out[...] = jnp.where(
        lane == 2, jnp.broadcast_to(flipped[rows - 1 : rows], (8, LANES)), 0.0
    )
    decay_all[mg] = decay_out[...]

    for load in (loads[0], loads[1], *loads[5:9]):
        load.wait()
    s_pad[RIM:] = state_in[...].astype(f32)
    s_conv[HEAD:] = conv_rows(
        s_pad, taps_s, bias_s, HEAD, rows - HEAD, slice(None)
    ).astype(bf16)
    for i in range(tiles):
        c = slice(i * LANES, (i + 1) * LANES)
        x_pad[RIM:, c] = x_in[:, c].astype(f32)
        x_conv[HEAD:, c] = conv_rows(
            x_pad, taps_x[:, c], bias_x[i : i + 1], HEAD, rows - HEAD, c
        ).astype(bf16)

    ahead = jnp.where(me < n - g, 1, 0)
    edge = jnp.where((mg == g - 1) & (me < n - 1), 1, 0)
    pl.semaphore_wait(barrier, g + ahead + edge)

    def rim_copies():
        target = {"seq": lax.rem(me + 1, n)}
        return [
            remote(
                src.at[pl.ds(rows - RIM, RIM)], dst, rim_send.at[i], rim_recv.at[i],
                target,
            )
            for i, (src, dst) in enumerate(((x_in, rim_x), (state_in, rim_s)))
        ]

    @pl.when(me < n - 1)
    def _():
        for copy in rim_copies():
            copy.start()

    def decay_start(k, _):
        remote(
            decay_out, decay_all.at[mg], d_send, d_recv,
            {"seq": base + lax.rem(mg + k, g)},
        ).start()
        return 0

    lax.fori_loop(1, g, decay_start, 0)

    towards = jnp.where(lane == 1, cols[...], 0.0)
    keys_main = s_conv[HEAD:, :NSTATE]
    for i in range(tiles):
        c = slice(i * LANES, (i + 1) * LANES)
        scaled = (
            x_conv[HEAD:, c].astype(f32) * spread_heads(towards[HEAD:], spread[:, c])
        ).astype(bf16)
        main[:, c] = lax.dot_general(
            keys_main, scaled, (((0,), (0,)), ((), ())), preferred_element_type=f32
        )

    loads[11].wait()
    for i in range(tiles):
        c = slice(i * LANES, (i + 1) * LANES)
        gate_act[:, c] = silu(gate_in[:, c].astype(f32))

    @pl.when(me > 0)
    def _():
        for copy in rim_copies():
            copy.wait_recv()
        s_pad[0:RIM] = rim_s[...].astype(f32)
        x_pad[0:RIM] = rim_x[...].astype(f32)

    @pl.when(me == 0)
    def _():
        s_pad[0:RIM] = jnp.zeros((RIM, s_pad.shape[1]), f32)
        x_pad[0:RIM] = jnp.zeros((RIM, inner), f32)

    s_conv[0:HEAD] = conv_rows(s_pad, taps_s, bias_s, 0, HEAD, slice(None)).astype(bf16)
    keys_head = s_conv[0:HEAD, :NSTATE]
    for (start, width), (out, got, *_) in zip(columns, part_refs):
        for i in range(start // LANES, (start + width) // LANES):
            c = slice(i * LANES, (i + 1) * LANES)
            at = slice(i * LANES - start, (i + 1) * LANES - start)
            x_head = conv_rows(
                x_pad, taps_x[:, c], bias_x[i : i + 1], 0, HEAD, c
            ).astype(bf16)
            x_conv[0:HEAD, c] = x_head
            scaled = (
                x_head.astype(f32) * spread_heads(towards[0:HEAD], spread[:, c])
            ).astype(bf16)
            out[:, at] = (
                main[:, c]
                + lax.dot_general(
                    keys_head, scaled, (((0,), (0,)), ((), ())),
                    preferred_element_type=f32,
                )
            ).astype(bf16)

    def own_rows(j):
        return pl.ds(pl.multiple_of(j * per, per), per)

    for b, (out, got, *_) in enumerate(part_refs):

        def state_start(k, _, b=b, out=out, got=got):
            to = lax.rem(mg + k, g)
            remote(
                out.at[own_rows(to)], got.at[mg], s1_send.at[b], s1_recv.at[b],
                {"seq": base + to},
            ).start()
            return 0

        lax.fori_loop(1, g, state_start, 0)
        got[mg] = out[own_rows(mg)]

    keys = s_conv[:, :NSTATE]
    query = s_conv[:, NSTATE:]
    causal = (
        lax.broadcasted_iota(jnp.int32, (rows, rows), 0)
        >= lax.broadcasted_iota(jnp.int32, (rows, rows), 1)
    )
    scores[...] = jnp.where(
        causal,
        lax.dot_general(
            query, keys, (((1,), (1,)), ((), ())), preferred_element_type=f32
        ),
        0.0,
    )
    first_half = lax.broadcasted_iota(jnp.int32, (1, LANES), 1) < HEAD_DIM
    loads[9].wait()

    def inside(i):
        c = slice(i * LANES, (i + 1) * LANES)
        x_c = x_conv[:, c]
        tops, bottoms = [], []
        for h in (2 * i, 2 * i + 1):
            a_row = shifted[h : h + 1, :]
            top = cols[0:half, h : h + 1] - a_row[:, :half]
            top = scores[0:half, 0:half] * jnp.exp(jnp.minimum(top, 80.0))
            tops.append(
                jnp.dot(top.astype(bf16), x_c[:half], preferred_element_type=f32)
            )
            low = cols[half:, h : h + 1] - a_row
            low = scores[half:, :] * jnp.exp(jnp.minimum(low, 80.0))
            bottoms.append(jnp.dot(low.astype(bf16), x_c, preferred_element_type=f32))
        gain = jnp.where(
            first_half,
            skip_gain[:, 2 * i : 2 * i + 1],
            skip_gain[:, 2 * i + 1 : 2 * i + 2],
        )
        x_f = x_c.astype(f32)
        mixed[0:half, c] = jnp.where(first_half, *tops) + gain * x_f[:half]
        mixed[half:, c] = jnp.where(first_half, *bottoms) + gain * x_f[half:]

    for i in range(tiles):
        inside(i)

    carry_decay = jnp.where(lane == 2, cols[...], 0.0)
    for i in range(tiles):
        c = slice(i * LANES, (i + 1) * LANES)
        decayed[:, c] = spread_heads(carry_decay, spread[:, c])

    wait_for(decay_all.at[pl.ds(0, g - 1)], d_recv)
    decay_cols[...] = spread_heads(
        decay_all[...].reshape(g * 8, LANES), spread[...]
    ).reshape(g, 8, inner)
    loads[10].wait()

    def send_on(b):
        _, _, _, back, ent, passing, coming = part_refs[b]

        @pl.when(me < n - g)
        def _():
            remote(
                passing, coming, c_send.at[b], c_recv.at[b], {"seq": me + g}
            ).start()

        def back_start(k, _):
            to = lax.rem(mg + k, g)

            @pl.when(base + to > 0)
            def _():
                remote(
                    back.at[to], ent.at[own_rows(mg)], s2_send.at[b], s2_recv.at[b],
                    {"seq": base + to},
                ).start()

            return 0

        lax.fori_loop(1, g, back_start, 0)
        ent[own_rows(mg)] = back[mg]

    for b, (start, width) in enumerate(columns):
        _, got, before, back, ent, passing, coming = part_refs[b]
        c = slice(start, start + width)
        wait_for(got.at[pl.ds(0, g - 1)], s1_recv.at[b])
        state = jnp.zeros((per, width), f32)
        for j in range(g):
            before[j] = state
            back[j] = state.astype(bf16)
            state = decay_cols[j][0:1, c] * state + got[j].astype(f32)
        before[g] = state
        passing[...] = state.astype(bf16)

        @pl.when(base == 0)
        def _(b=b):
            send_on(b)

        if b == 0:

            @pl.when(base > 0)
            def _():
                reached = jnp.ones((8, inner), f32)
                for j in range(g):
                    reach[j] = reached
                    reached = reached * decay_cols[j]
                reach[g] = reached

    @pl.when(base > 0)
    def _():
        for b, (start, width) in enumerate(columns):
            _, got, before, back, ent, passing, coming = part_refs[b]
            c = slice(start, start + width)
            remote(
                passing, coming, c_send.at[b], c_recv.at[b], {"seq": me - g}
            ).wait_recv()
            entered = coming[...].astype(f32)
            for j in range(g):
                back[j] = (before[j] + reach[j][0:1, c] * entered).astype(bf16)
            passing[...] = (before[g] + reach[g][0:1, c] * entered).astype(bf16)
            send_on(b)

    @pl.when(me == 0)
    def _():
        ent0[...] = jnp.zeros_like(ent0)
        ent1[...] = jnp.zeros_like(ent1)

    loads[12].wait()

    def across(src, dst, send, recv):
        return remote(src, dst, send, recv, {"tp": other})

    pieces, _, width = part.shape

    def part_copy(p):
        return across(part.at[p], part_got.at[p], o_send.at[p], o_recv.at[p])

    copy_q = across(squares, squares_got, q_sem.at[0], q_sem.at[1])
    total = jnp.zeros((rows, LANES), f32)
    last = len(columns) - 1
    for b, (start, size) in enumerate(columns):
        ent = part_refs[b][4]

        @pl.when(me > 0)
        def _(b=b, ent=ent):
            wait_for(ent.at[pl.ds(0, (g - 1) * per)], s2_recv.at[b])

        for i in range(start // LANES, (start + size) // LANES):
            c = slice(i * LANES, (i + 1) * LANES)
            carried = jnp.dot(
                query, ent[:, i * LANES - start : (i + 1) * LANES - start],
                preferred_element_type=f32,
            )
            raw = (mixed[:, c] + carried * decayed[:, c]) * gate_act[:, c]
            total = total + raw * raw
            gated[:, c] = (raw * norm_gain[i : i + 1]).astype(bf16)
        if b == last:
            squares[...] = total
            copy_q.start()
        c = slice(start, start + size)
        for side in (0, 1):
            owner = other if side == 0 else core
            for p in range(pieces):
                at = pl.ds(pl.multiple_of(owner * inner + p * width, LANES), width)
                value = jnp.dot(
                    gated[:, c], w_all[c, at], preferred_element_type=f32
                )
                if b > 0:
                    value = value + acc[side, p]
                if b == last and side == 0:
                    part[p] = value.astype(bf16)
                    part_copy(p).start()
                else:
                    acc[side, p] = value
    copy_q.wait_recv()
    both = jnp.sum(squares[...] + squares_got[...], axis=1, keepdims=True)
    scale = lax.rsqrt(both / (2 * inner) + 1e-05)
    for p in range(pieces):
        part_copy(p).wait_recv()
        out_ref[:, p * width : (p + 1) * width] = (
            (acc[1, p] + part_got[p].astype(f32)) * scale
        ).astype(bf16)

    copy_q.wait_send()
    for p in range(pieces):
        part_copy(p).wait_send()
    wait_for(decay_all.at[pl.ds(0, g - 1)], d_send)

    @pl.when(me < n - 1)
    def _():
        for copy in rim_copies():
            copy.wait_send()

    for b in range(len(columns)):
        out, got, before, back, ent, passing, coming = part_refs[b]
        wait_for(got.at[pl.ds(0, g - 1)], s1_send.at[b])

        @pl.when((base > 0) | (me == 0))
        def _(b=b, back=back):
            wait_for(back.at[pl.ds(0, g - 1)], s2_send.at[b])

        @pl.when((base == 0) & (me > 0))
        def _(b=b, back=back):
            wait_for(back.at[pl.ds(0, g - 2)], s2_send.at[b])

        @pl.when(me < n - g)
        def _(b=b, passing=passing, coming=coming):
            remote(
                passing, coming, c_send.at[b], c_recv.at[b], {"seq": me + g}
            ).wait_send()


def local(
    inner_input, gate_input, state_input, step_raw, conv_inner, conv_state,
    bias_inner, bias_state, step_bias, decay_log, skip_gain, norm_gain, out_weight,
):
    n = lax.axis_size("seq")
    g = math.gcd(n, 8)
    per = NSTATE // g
    rows, inner = inner_input.shape
    maps = state_input.shape[1]
    width = 256
    pieces = inner // width
    (_, w0), (_, w1) = split_columns(inner)
    vm = pltpu.VMEM
    dma = pltpu.SemaphoreType.DMA
    row = lambda v: v.reshape(1, -1)
    tile = lambda v: v.reshape(-1, LANES)
    operands = (
        inner_input, gate_input, state_input, step_raw, conv_inner, conv_state,
        tile(bias_inner), row(bias_state), row(step_bias), row(decay_log),
        row(skip_gain), tile(norm_gain), out_weight,
    )
    scratch = [vm(v.shape, v.dtype) for v in operands]
    scratch += [
        vm((rows + RIM, inner), f32),
        vm((rows + RIM, maps), f32),
        vm((rows, inner), bf16),
        vm((rows, maps), bf16),
        vm((LANES, rows), f32),
        vm((LANES, inner), bf16),
        vm((rows, LANES), f32),
        vm((rows, rows), f32),
        vm((rows, inner), f32),
        vm((rows, inner), f32),
        vm((rows, inner), f32),
        vm((rows, inner), bf16),
        vm((NSTATE, inner), f32),
        vm((RIM, inner), bf16),
        vm((RIM, maps), bf16),
        vm((8, LANES), f32),
        vm((g, 8, LANES), f32),
        vm((g, 8, inner), f32),
        vm((g + 1, 8, inner), f32),
    ]
    for shape, dtype in (
        ((NSTATE,), bf16), ((g, per), bf16), ((g + 1, per), f32), ((g, per), bf16),
        ((NSTATE,), bf16), ((per,), bf16), ((per,), bf16),
    ):
        scratch += [vm((*shape, w0), dtype), vm((*shape, w1), dtype)]
    scratch += [
        vm((2, pieces, rows, width), f32),
        vm((pieces, rows, width), bf16),
        vm((pieces, rows, width), bf16),
        vm((rows, LANES), f32),
        vm((rows, LANES), f32),
        dma((len(operands),)), dma((2,)), dma((2,)), dma, dma,
        dma((2,)), dma((2,)), dma((2,)), dma((2,)), dma((2,)), dma((2,)),
        dma((pieces,)), dma((pieces,)), dma((2,)),
    ]
    return pl.pallas_call(
        functools.partial(kernel, n, g),
        out_shape=pltpu.VMEM((rows, inner), bf16),
        in_specs=[pl.BlockSpec(memory_space=pltpu.HBM)] * len(operands),
        out_specs=pl.BlockSpec(memory_space=pltpu.VMEM),
        scratch_shapes=scratch,
        compiler_params=pltpu.CompilerParams(
            collective_id=0, has_side_effects=True, vmem_limit_bytes=58 * 2**20
        ),
        name="ssd_block",
    )(*operands)


def solution(mesh):
    return jax.shard_map(
        local,
        mesh=mesh,
        in_specs=(
            P("seq", "tp"),
            P("seq", "tp"),
            P("seq", None),
            P("tp", "seq"),
            P(None, "tp"),
            P(),
            P("tp"),
            P(),
            P("tp"),
            P("tp"),
            P("tp"),
            P("tp"),
            P("tp", None),
        ),
        out_specs=P("seq", "tp"),
        check_vma=False,
    )
```

time: 37 us -> 26.8 us (0.72)
  the two profiles are of different devices: /device:TPU:3 before, /device:TPU:17 now
where the time goes in v1:
time: 26.8 us; the launch traced here: 26.3 us
  Pallas kernels  25.4 us (95%)
  local copies, waits for them, and re-layouts  0.84 us (3%)
    pallas_call x1, Pallas kernels, local(): pl.pallas_call(functools.partial(kernel, n, g), out_shape=pltpu.VMEM((row...  25.4 us
    unnamed x1, local copies, waits for them, and re-layouts  0.84 us

profile of v1, /device:TPU:17, one launch (start us, length us, event | category | flops | bytes accessed | tf_op | source)
XLA Modules:
  0.0 26.3 jit_solution(16837430341920132113)
XLA Ops:
  0.0 25.4 %ssd_block.1 = bf16[256,1280]{1,0:T(8,128)(2,1)S(1)} custom-call(bf16[256,1280]{1,0:T(8,128)(2,1)} %x_hbm.1, bf16[256,1280]{1,0:T(8,128)(2,1)} %gate_hbm.1, bf16[256,256]{1,0:T(8,128)(2,1)} %state_hbm.1, f32[20,256]{1,0:T(8,128)} %step_hbm.1, f32[4,1280]{1,0:T(4,128)} %taps_x_hbm.1, f32[4,256]{1,0:T(4,128)} %taps_s_hbm.1, f32[10,128]{1,0:T(8,128)} %bitcast.6, ...), custom_call_target="tpu_custom_call" | custom-call | tf_op jit(solution)/shard_map/ssd_block/pallas_call | solution.py:553
  25.4 0.8 %copy.15 = bf16[256,1280]{1,0:T(8,128)(2,1)} copy(bf16[256,1280]{1,0:T(8,128)(2,1)S(1)} %ssd_block.1) | data formatting | bytes 1310720
